TPU v7x, 32 devices: a whole 2x2x4 slice. The times are simulated.
32 devices in a mesh: tm: 16 (over z, y, core), user: 2 (over x).
Axes of the slice: x: 2, y: 2, z: 4, core: 2. Of those that a mesh axis runs over, the one named last changes fastest.
Arguments:
- events: bfloat16 [64, 1024, 256], P('user', 'tm'), parts along dimension 0, may hold values from -6 to 6
- lengths: int32 [64], P('user'), parts along dimension 0, may hold values from 256 to 1024
- w_mix: bfloat16 [2, 256, 256], replicated, may hold values from -0.375 to 0.375
- w_context: bfloat16 [2, 256, 256], replicated, may hold values from -0.375 to 0.375
- gains: float32 [2, 256], replicated, may hold values from 0.5 to 1.5
- w_up: bfloat16 [2, 256, 1024], replicated, may hold values from -0.375 to 0.375
- w_down: bfloat16 [2, 1024, 256], replicated, may hold values from -0.1875 to 0.1875
Outputs:
- encoded: bfloat16 [64, 1024, 256], P('user', 'tm'), parts along dimension 0
There are 2 independent parts, one for each index of `user`. A program takes and returns all parts, laid end to end along the dimension named above; an argument that names none is the same for every part. Nothing has to cross between parts.
All inputs are finite; a program needn't handle non-finite values.
Results may differ from a plain program's by a relative error of at most 0.012.
Values may be sent and summed in bfloat16 or wider, within the bound.
A program may use at most 64 MiB of HBM per device.

v0:
```python
import jax
import jax.numpy as jnp
from jax import lax
from jax.sharding import PartitionSpec as P

D = 256
HALF = 32
LAYERS = 2


def with_halo(block, sides, width):
    for axis, dim in sides:
        count = lax.axis_size(axis)
        forward = [(i, i + 1) for i in range(count - 1)]
        backward = [(target, source) for source, target in forward]
        low = lax.ppermute(
            lax.slice_in_dim(block, block.shape[dim] - width, None, axis=dim), axis, forward
        )
        high = lax.ppermute(lax.slice_in_dim(block, 0, width, axis=dim), axis, backward)
        block = jnp.concatenate([low, block, high], axis=dim)
    return block


def earlier_sums(totals):
    my_index = lax.axis_index("tm")
    pieces = lax.all_gather(totals[None], "tm", axis=0, tiled=True)
    shard_order = jnp.arange(pieces.shape[0], dtype=jnp.int32)
    keep_mask = (shard_order < my_index)[:, None, None]
    return jnp.sum(jnp.where(keep_mask, pieces, 0.0), axis=0)


def per_device(events, lengths, w_mix, w_context, gains, w_up, w_down):
    own_rows = events.shape[1]
    first_pos = lax.axis_index("tm") * own_rows

    def valid_at(row_count):
        position = first_pos + jnp.arange(row_count, dtype=jnp.int32)
        return (position[None, :] >= 0) & (position[None, :] < lengths[:, None])

    current = jnp.where(valid_at(own_rows)[..., None], events, jnp.zeros_like(events))
    for layer_index in range(LAYERS):
        extended = with_halo(current, (("tm", 1),), HALF)
        own_part = current
        totals = jnp.sum(own_part, axis=1, dtype=jnp.float32)
        earlier = earlier_sums(totals)
        before = jnp.sum(current[:, :0], axis=1, dtype=jnp.float32)
        context_row_count = current.shape[1]
        index_rows = jnp.arange(context_row_count, dtype=jnp.int32)
        lower_ones = (index_rows[:, None] >= index_rows[None, :]).astype(jnp.bfloat16)
        running = jnp.einsum("ts,usd->utd", lower_ones, current, preferred_element_type=jnp.float32)
        running = running + (earlier - before)[:, None, :]
        context_position = (first_pos - 0 + index_rows).astype(jnp.float32)
        scale = 1.0 / jnp.sqrt(jnp.maximum(context_position + 1.0, 1.0))
        context = (running * scale[None, :, None]).astype(jnp.bfloat16)
        apply_row_count = extended.shape[1] - 2 * HALF
        center = extended[:, HALF : HALF + apply_row_count]
        scores = (
            jnp.einsum("utd,usd->uts", center, extended, preferred_element_type=jnp.float32) / D
        )
        target = jnp.arange(apply_row_count, dtype=jnp.int32)[:, None]
        source = jnp.arange(extended.shape[1], dtype=jnp.int32)[None, :]
        in_band = (source >= target) & (source <= target + 2 * HALF)
        weights = jnp.where(in_band[None], scores, 0.0).astype(jnp.bfloat16)
        mixed_rows = jnp.einsum(
            "uts,usd->utd", weights, extended, preferred_element_type=jnp.float32
        ).astype(jnp.bfloat16)
        compressed = jnp.dot(mixed_rows, w_mix[layer_index], preferred_element_type=jnp.float32)
        compressed = compressed + jnp.dot(
            context, w_context[layer_index], preferred_element_type=jnp.float32
        )
        summed = center.astype(jnp.float32) + compressed
        row_mean = jnp.mean(summed, axis=-1, keepdims=True)
        row_var = jnp.mean((summed - row_mean) ** 2, axis=-1, keepdims=True)
        normed = ((summed - row_mean) / jnp.sqrt(row_var + 1e-05) * gains[layer_index]).astype(
            jnp.bfloat16
        )
        hidden = jax.nn.relu(
            jnp.dot(normed, w_up[layer_index], preferred_element_type=jnp.float32)
        ).astype(jnp.bfloat16)
        result = normed.astype(jnp.float32) + jnp.dot(
            hidden, w_down[layer_index], preferred_element_type=jnp.float32
        )
        valid_mask = valid_at(apply_row_count)
        current = jnp.where(valid_mask[..., None], result, 0.0).astype(jnp.bfloat16)
    return current


def solution(mesh):
    placed = (P("user", "tm", None), P("user"), P(), P(), P(), P(), P())
    return jax.shard_map(
        per_device, mesh=mesh, in_specs=placed, out_specs=P("user", "tm", None), check_vma=False
    )
```

profile of v0, /device:TPU:0, one launch (start us, length us, event | category | flops | bytes accessed | tf_op | source)
XLA Modules:
  0.0 86.9 jit_solution(9084235263764099219)
XLA Ops:
  0.0 0.7 compare_and_fusion
  0.7 1.6 %convert_reduce_fusion.1 = (f32[32,256]{1,0:T(8,128)S(1)}, bf16[32,64,256]{2,1,0:T(8,128)(2,1)S(1)}) fusion(bf16[32,64,256]{2,1,0:T(8,128)(2,1)} %param.7, pred[32,64]{1,0:T(8,128)(4,1)S(1)} %compare_and_fusion), kind=kLoop, calls=%fused_computation.11 | loop fusion | flops 1564672 | bytes 2131968 | tf_op jit(solution)/shard_map/reduce_sum | solution.py:44
  2.3 0.1 fusion.71
  2.4 2.4 %collective-permute-start = (bf16[32,32,256]{2,1,0:T(8,128)(2,1)S(1)}, bf16[32,32,256]{2,1,0:T(8,128)(2,1)S(1)}, u32[]{:S(2)}, u32[]{:S(2)}) collective-permute-start(bf16[32,32,256]{2,1,0:T(8,128)(2,1)S(1)} %get-tuple-element.9), channel_id=1, source_target_pairs={{0,2},{2,4},{4,6},{6,8},{8,10},{10,12},{12,14},{14,16},{16,18},{18... | collective-permute-start | bytes 1572872 | tf_op jit(solution)/shard_map/ppermute | solution.py:16
  4.8 1.3 %collective-permute-start.1 = (bf16[32,32,256]{2,1,0:T(8,128)(2,1)S(1)}, bf16[32,32,256]{2,1,0:T(8,128)(2,1)S(1)}, u32[]{:S(2)}, u32[]{:S(2)}) collective-permute-start(bf16[32,32,256]{2,1,0:T(8,128)(2,1)S(1)} %get-tuple-element.10), channel_id=1, source_target_pairs={{2,0},{4,2},{6,4},{8,6},{10,8},{12,10},{14,12},{16,14},{18,16},{20... | collective-permute-start | bytes 1572872 | tf_op jit(solution)/shard_map/ppermute | solution.py:19
  6.2 28.2 %all-gather = f32[512,256]{1,0:T(8,128)S(1)} all-gather(f32[32,256]{1,0:T(8,128)S(1)} %get-tuple-element.5), channel_id=2, replica_groups=mesh['tm'=16,'user'=2] {'tm'}, dimensions={0}, use_global_device_ids=true | all-gather | bytes 557056 | tf_op jit(solution)/shard_map/all_gather | solution.py:26
  34.3 0.1 select_reduce_fusion.1
  34.5 0.1 fusion.56
  34.6 0.8 fusion.19
  35.5 2.1 %fusion.12 = f32[32,64,256]{2,1,0:T(8,128)} fusion(bf16[32,64,128]{2,1,0:T(8,128)(2,1)S(1)} %fusion.19, bf16[32,32,256]{2,1,0:T(8,128)(2,1)S(1)} %collective-permute-done.1, bf16[32,64,256]{2,1,0:T(8,128)(2,1)S(1)} %get-tuple-element.6, bf16[32,32,256]{2,1,0:T(8,128)(2,1)S(1)} %collective-permute-done, bf16[2,256,256]{2,1,0:T(8,128)(2,1)S(1)} %copy-done.4), kind=kOutput, calls=%fused_computation.28 | convolution fusion | flops 409468928 | bytes 4849664 | tf_op jit(solution)/shard_map/dot_general | solution.py:67
  37.6 2.5 %fusion.73 = (f32[32,64]{1,0:T(8,128)S(1)}, f32[32,64,256]{2,1,0:T(8,128)S(1)}) fusion(f32[32,64,256]{2,1,0:T(8,128)} %fusion.12, bf16[2,256,256]{2,1,0:T(8,128)(2,1)S(1)} %copy-done.1, bf16[32,64,256]{2,1,0:T(8,128)(2,1)S(1)} %get-tuple-element.6, f32[64]{0:T(128)S(1)} %maximum_rsqrt_fusion, f32[32,256]{1,0:T(8,128)S(1)} %select_reduce_fusion.1), kind=kOutput, calls=%fused_computation.89 | convolution fusion | flops 339216384 | bytes 6464000 | tf_op jit(solution)/shard_map/dot_general | solution.py:68
  40.1 0.6 multiply_reduce_fusion.1
  40.8 4.0 %convert_reduce_fusion = (f32[32,256]{1,0:T(8,128)S(1)}, bf16[32,64,256]{2,1,0:T(8,128)(2,1)S(1)}) fusion(bf16[2,1024,256]{2,1,0:T(8,128)(2,1)} %param.13, f32[32,64,256]{2,1,0:T(8,128)S(1)} %get-tuple-element.14, f32[256]{0:T(256)S(1)} %bitcast.77, f32[32,64]{1,0:T(8,128)S(1)} %add_sqrt_fusion.1, f32[32,64]{1,0:T(8,128)S(1)} %broadcast_multiply_fusion.1, ...), kind=kOutput, calls=%fused_computation.9 | convolution fusion | flops 2159009792 | bytes 6395904 | tf_op jit(solution)/shard_map/dot_general | solution.py:80
  44.8 0.1 fusion.70
  44.9 2.3 %collective-permute-start.2 = (bf16[32,32,256]{2,1,0:T(8,128)(2,1)S(1)}, bf16[32,32,256]{2,1,0:T(8,128)(2,1)S(1)}, u32[]{:S(2)}, u32[]{:S(2)}) collective-permute-start(bf16[32,32,256]{2,1,0:T(8,128)(2,1)S(1)} %get-tuple-element.7), channel_id=1, source_target_pairs={{0,2},{2,4},{4,6},{6,8},{8,10},{10,12},{12,14},{14,16},{16,18},{18... | collective-permute-start | bytes 1572872 | tf_op jit(solution)/shard_map/ppermute | solution.py:16
  47.2 1.3 %collective-permute-start.3 = (bf16[32,32,256]{2,1,0:T(8,128)(2,1)S(1)}, bf16[32,32,256]{2,1,0:T(8,128)(2,1)S(1)}, u32[]{:S(2)}, u32[]{:S(2)}) collective-permute-start(bf16[32,32,256]{2,1,0:T(8,128)(2,1)S(1)} %get-tuple-element.8), channel_id=1, source_target_pairs={{2,0},{4,2},{6,4},{8,6},{10,8},{12,10},{14,12},{16,14},{18,16},{20... | collective-permute-start | bytes 1572872 | tf_op jit(solution)/shard_map/ppermute | solution.py:19
  48.5 26.3 %all-gather.1 = f32[512,256]{1,0:T(8,128)S(1)} all-gather(f32[32,256]{1,0:T(8,128)S(1)} %get-tuple-element.15), channel_id=3, replica_groups=mesh['tm'=16,'user'=2] {'tm'}, dimensions={0}, use_global_device_ids=true | all-gather | bytes 557056 | tf_op jit(solution)/shard_map/all_gather | solution.py:26
  74.8 0.1 select_reduce_fusion
  74.9 0.8 fusion.17
  75.8 2.1 %fusion.13 = f32[32,64,256]{2,1,0:T(8,128)} fusion(bf16[32,64,128]{2,1,0:T(8,128)(2,1)S(1)} %fusion.17, bf16[32,32,256]{2,1,0:T(8,128)(2,1)S(1)} %collective-permute-done.3, bf16[32,64,256]{2,1,0:T(8,128)(2,1)S(1)} %get-tuple-element.16, bf16[32,32,256]{2,1,0:T(8,128)(2,1)S(1)} %collective-permute-done.2, bf16[2,256,256]{2,1,0:T(8,128)(2,1)S(1)} %copy-done.5), kind=kOutput, calls=%fused_computation.29 | convolution fusion | flops 409468928 | bytes 4849664 | tf_op jit(solution)/shard_map/dot_general | solution.py:67
  77.9 3.0 %fusion.78 = (f32[32,64]{1,0:T(8,128)S(1)}, f32[32,64,256]{2,1,0:T(8,128)S(1)}) fusion(f32[32,64,256]{2,1,0:T(8,128)} %fusion.13, bf16[2,256,256]{2,1,0:T(8,128)(2,1)S(1)} %copy-done.1, bf16[32,64,256]{2,1,0:T(8,128)(2,1)} %copy-done, f32[32,256]{1,0:T(8,128)S(1)} %select_reduce_fusion, f32[64]{0:T(128)S(1)} %maximum_rsqrt_fusion), kind=kOutput, calls=%fused_computation.90 | convolution fusion | flops 339216384 | bytes 6464000 | tf_op jit(solution)/shard_map/dot_general | solution.py:68
  81.0 0.6 multiply_reduce_fusion
  81.7 0.5 copy-done.3
  82.2 4.7 %select_convert_fusion = bf16[32,64,256]{2,1,0:T(8,128)(2,1)} fusion(f32[32,64,256]{2,1,0:T(8,128)S(1)} %get-tuple-element.18, f32[256]{0:T(256)S(1)} %bitcast.76, f32[32,64]{1,0:T(8,128)S(1)} %add_sqrt_fusion, f32[32,64]{1,0:T(8,128)S(1)} %broadcast_multiply_fusion, pred[32,64]{1,0:T(8,128)(4,1)S(1)} %compare_and_fusion, ...), kind=kOutput, calls=%fused_computation.14 | convolution fusion | flops 2157969408 | bytes 6363136 | tf_op jit(solution)/shard_map/dot_general | solution.py:80
  (25 shorter events, 0.2 us)
Async XLA Ops:
  2.3 32.2 %copy-start.2 = (f32[2,256]{1,0:T(2,128)S(1)}, f32[2,256]{1,0:T(2,128)}, u32[]{:S(2)}) copy-start(f32[2,256]{1,0:T(2,128)} %param.11) | copy-start | bytes 6148
  2.4 32.2 %collective-permute-start = (bf16[32,32,256]{2,1,0:T(8,128)(2,1)S(1)}, bf16[32,32,256]{2,1,0:T(8,128)(2,1)S(1)}, u32[]{:S(2)}, u32[]{:S(2)}) collective-permute-start(bf16[32,32,256]{2,1,0:T(8,128)(2,1)S(1)} %get-tuple-element.9), channel_id=1, source_target_pairs={{0,2},{2,4},{4,6},{6,8},{8,10},{10,12},{12,14},{14,16},{16,18},{18... | collective-permute-start | bytes 1572872 | tf_op jit(solution)/shard_map/ppermute | solution.py:16
  4.8 29.7 %collective-permute-start.1 = (bf16[32,32,256]{2,1,0:T(8,128)(2,1)S(1)}, bf16[32,32,256]{2,1,0:T(8,128)(2,1)S(1)}, u32[]{:S(2)}, u32[]{:S(2)}) collective-permute-start(bf16[32,32,256]{2,1,0:T(8,128)(2,1)S(1)} %get-tuple-element.10), channel_id=1, source_target_pairs={{2,0},{4,2},{6,4},{8,6},{10,8},{12,10},{14,12},{16,14},{18,16},{20... | collective-permute-start | bytes 1572872 | tf_op jit(solution)/shard_map/ppermute | solution.py:19
  34.6 1.0 %copy-start.4 = (bf16[2,256,256]{2,1,0:T(8,128)(2,1)S(1)}, bf16[2,256,256]{2,1,0:T(8,128)(2,1)}, u32[]{:S(2)}) copy-start(bf16[2,256,256]{2,1,0:T(8,128)(2,1)} %param.9) | copy-start | bytes 786436
  35.5 2.1 %copy-start.1 = (bf16[2,256,256]{2,1,0:T(8,128)(2,1)S(1)}, bf16[2,256,256]{2,1,0:T(8,128)(2,1)}, u32[]{:S(2)}) copy-start(bf16[2,256,256]{2,1,0:T(8,128)(2,1)} %param.10) | copy-start | bytes 786436
  44.8 31.0 %copy-start = (bf16[32,64,256]{2,1,0:T(8,128)(2,1)}, bf16[32,64,256]{2,1,0:T(8,128)(2,1)S(1)}, u32[]{:S(2)}) copy-start(bf16[32,64,256]{2,1,0:T(8,128)(2,1)S(1)} %get-tuple-element.16) | copy-start | bytes 3145732
  44.9 30.0 %collective-permute-start.2 = (bf16[32,32,256]{2,1,0:T(8,128)(2,1)S(1)}, bf16[32,32,256]{2,1,0:T(8,128)(2,1)S(1)}, u32[]{:S(2)}, u32[]{:S(2)}) collective-permute-start(bf16[32,32,256]{2,1,0:T(8,128)(2,1)S(1)} %get-tuple-element.7), channel_id=1, source_target_pairs={{0,2},{2,4},{4,6},{6,8},{8,10},{10,12},{12,14},{14,16},{16,18},{18... | collective-permute-start | bytes 1572872 | tf_op jit(solution)/shard_map/ppermute | solution.py:16
  47.2 27.7 %collective-permute-start.3 = (bf16[32,32,256]{2,1,0:T(8,128)(2,1)S(1)}, bf16[32,32,256]{2,1,0:T(8,128)(2,1)S(1)}, u32[]{:S(2)}, u32[]{:S(2)}) collective-permute-start(bf16[32,32,256]{2,1,0:T(8,128)(2,1)S(1)} %get-tuple-element.8), channel_id=1, source_target_pairs={{2,0},{4,2},{6,4},{8,6},{10,8},{12,10},{14,12},{16,14},{18,16},{20... | collective-permute-start | bytes 1572872 | tf_op jit(solution)/shard_map/ppermute | solution.py:19
  74.9 1.0 %copy-start.5 = (bf16[2,256,256]{2,1,0:T(8,128)(2,1)S(1)}, bf16[2,256,256]{2,1,0:T(8,128)(2,1)}, u32[]{:S(2)}) copy-start(bf16[2,256,256]{2,1,0:T(8,128)(2,1)} %param.9) | copy-start | bytes 786436
  81.0 1.2 %copy-start.3 = (bf16[2,1024,256]{2,1,0:T(8,128)(2,1)S(1)}, bf16[2,1024,256]{2,1,0:T(8,128)(2,1)}, u32[]{:S(2)}) copy-start(bf16[2,1024,256]{2,1,0:T(8,128)(2,1)} %param.13) | copy-start | bytes 3145732
where the time goes:
time: 87.3 us; the launch traced here: 86.9 us
  blocking collectives  54.4 us (62%)
  matrix products  20.1 us (23%)
  starting transfers between devices  7.29 us (8%)
  other arithmetic  3.92 us (4%)
    all_gather x2, blocking collectives, earlier_sums(): pieces = lax.all_gather(totals[None], 'tm', axis=0, tiled=True)  54.4 us
    dot_general x2, matrix products, per_device(): jnp.dot(hidden, w_down[layer_index], preferred_element_type=jnp.float32)  8.65 us
    dot_general x2, matrix products, per_device(): jnp.dot(context, w_context[layer_index], preferred_element_type=jnp.float32)  5.5 us
    ppermute x2, starting transfers between devices, with_halo(): lax.ppermute(lax.slice_in_dim(block, block.shape[dim] - width, None, axis...  4.7 us
    dot_general x2, matrix products, per_device(): jnp.dot(mixed_rows, w_mix[layer_index], preferred_element_type=jnp.float32)  4.24 us
    ppermute x2, starting transfers between devices, with_halo(): lax.ppermute(lax.slice_in_dim(block, 0, width, axis=dim), axis, backward)  2.58 us
  transfers between devices with their start and end apart: 4, of which 0 were waited for; matrix products, arithmetic and copies ran while one was open for 0% of the time, Pallas kernels for 0%

commit v1 on v0

v1 whole, which is shorter than its diff:
```python
import functools

import jax
import jax.numpy as jnp
from jax import lax
from jax.experimental import pallas as pl
from jax.experimental.pallas import tpu as pltpu
from jax.sharding import PartitionSpec as P

HALF = 32
ROWS = 256
BLOCK = 8
EPS = 1e-05
MESH = pl.DeviceIdType.MESH


def group_size(count):
    size = 1
    while size * size < count:
        size *= 2
    return size if count % size == 0 else 1


def dot(a, b):
    return jnp.dot(a, b, preferred_element_type=jnp.float32)


def dot_t(a, b):
    return lax.dot_general(a, b, (((1,), (1,)), ((), ())), preferred_element_type=jnp.float32)


def kernel(
    count,
    lengths,
    gains,
    events,
    w_mix,
    w_context,
    w_up,
    w_down,
    out,
    x,
    result,
    low,
    high,
    mixed_own,
    mix_v,
    ctx_v,
    up_v,
    down_v,
    own_mask,
    halo_mask,
    lower_ones,
    row_scale,
    user_ones,
    totals,
    group_got,
    plane,
    cross_got,
    earlier,
    event_sem,
    weight_sem,
    out_sem,
    halo_send,
    halo_recv,
    group_send,
    group_recv,
    cross_send,
    cross_recv,
):
    layers, users, rows, width = x.shape
    steps = users // BLOCK
    per_dot = ROWS // rows
    me = lax.axis_index("tm")
    first_pos = me * rows
    group = group_got.shape[1] + 1
    groups = count // group
    in_group = lax.rem(me, group)
    my_group = lax.div(me, group)

    def event_copy(step):
        part = pl.ds(step * BLOCK, BLOCK)
        return pltpu.make_async_copy(events.at[part], x.at[0, part], event_sem.at[step])

    weight_copies = [
        pltpu.make_async_copy(source, target, weight_sem.at[i])
        for i, (source, target) in enumerate(
            ((w_mix, mix_v), (w_context, ctx_v), (w_up, up_v), (w_down, down_v))
        )
    ]
    for step in range(steps):
        event_copy(step).start()
    for copy in weight_copies:
        copy.start()

    barrier = pltpu.get_barrier_semaphore()

    def group_peer(k):
        return my_group * group + lax.rem(in_group + k, group)

    def cross_peer(k):
        return me + k * group

    for k in range(1, group):
        pl.semaphore_signal(barrier, inc=1, device_id={"tm": group_peer(k)}, device_id_type=MESH)
    for k in range(1, groups):
        other = lax.rem(me + k * group, count)
        pl.semaphore_signal(barrier, inc=1, device_id={"tm": other}, device_id_type=MESH)

    @pl.when(me > 0)
    def _():
        pl.semaphore_signal(barrier, inc=1, device_id={"tm": me - 1}, device_id_type=MESH)

    @pl.when(me < count - 1)
    def _():
        pl.semaphore_signal(barrier, inc=1, device_id={"tm": me + 1}, device_id_type=MESH)

    sides = (me > 0).astype(jnp.int32) + (me < count - 1).astype(jnp.int32)
    pl.semaphore_wait(barrier, group + groups - 2 + sides)

    def to_next(layer, step):
        part = pl.ds(step * BLOCK, BLOCK)
        source = events.at[part] if layer == 0 else x.at[layer, part]
        return pltpu.make_async_remote_copy(
            src_ref=source.at[:, pl.ds(rows - HALF, HALF)],
            dst_ref=low.at[layer, part],
            send_sem=halo_send.at[layer, 0, step],
            recv_sem=halo_recv.at[layer, 0, step],
            device_id={"tm": me + 1},
            device_id_type=MESH,
        )

    def to_previous(layer, step):
        part = pl.ds(step * BLOCK, BLOCK)
        source = events.at[part] if layer == 0 else x.at[layer, part]
        return pltpu.make_async_remote_copy(
            src_ref=source.at[:, pl.ds(0, HALF)],
            dst_ref=high.at[layer, part],
            send_sem=halo_send.at[layer, 1, step],
            recv_sem=halo_recv.at[layer, 1, step],
            device_id={"tm": me - 1},
            device_id_type=MESH,
        )

    def send_halos(layer, step):
        @pl.when(me < count - 1)
        def _():
            to_next(layer, step).start()

        @pl.when(me > 0)
        def _():
            to_previous(layer, step).start()

    def wait_halos(layer, step):
        @pl.when(me > 0)
        def _():
            to_next(layer, step).wait_recv()

        @pl.when(me < count - 1)
        def _():
            to_previous(layer, step).wait_recv()

    def wait_halo_sends(layer, step):
        @pl.when(me < count - 1)
        def _():
            to_next(layer, step).wait_send()

        @pl.when(me > 0)
        def _():
            to_previous(layer, step).wait_send()

    for step in range(steps):
        send_halos(0, step)

    row_bits, half_bits = rows.bit_length() - 1, HALF.bit_length() - 1
    target = lax.broadcasted_iota(jnp.int32, (ROWS, ROWS), 0)
    source = lax.broadcasted_iota(jnp.int32, (ROWS, ROWS), 1)
    target_user, source_user = target >> row_bits, source >> row_bits
    t, s = target & (rows - 1), source & (rows - 1)
    same = target_user == source_user
    near = (s - t <= HALF) & (t - s <= HALF)
    own_mask[...] = jnp.where(same & near, 1.0 / width, 0.0)
    lower_ones[...] = jnp.where(same & (s <= t), 1.0, 0.0).astype(jnp.bfloat16)
    side_rows = per_dot * HALF
    wide = 2 * side_rows
    target = lax.broadcasted_iota(jnp.int32, (ROWS, wide), 0)
    source = lax.broadcasted_iota(jnp.int32, (ROWS, wide), 1)
    is_high = source >= side_rows
    source = jnp.where(is_high, source - side_rows, source)
    s = (source & (HALF - 1)) + jnp.where(is_high, rows, -HALF)
    t = target & (rows - 1)
    same = (target >> row_bits) == (source >> half_bits)
    near = (s - t <= HALF) & (t - s <= HALF)
    halo_mask[...] = jnp.where(same & near, 1.0 / width, 0.0)
    position = first_pos + lax.broadcasted_iota(jnp.int32, (rows, width), 0)
    row_scale[...] = 1.0 / jnp.sqrt(position.astype(jnp.float32) + 1.0)
    user = lax.broadcasted_iota(jnp.int32, (BLOCK, BLOCK * rows), 0)
    row = lax.broadcasted_iota(jnp.int32, (BLOCK, BLOCK * rows), 1)
    user_ones[...] = jnp.where(user == (row >> row_bits), 1.0, 0.0).astype(jnp.bfloat16)

    @pl.when(me == 0)
    def _():
        low[...] = jnp.zeros_like(low)

    @pl.when(me == count - 1)
    def _():
        high[...] = jnp.zeros_like(high)

    def masked(block, step, start):
        offset = lax.broadcasted_iota(jnp.int32, block.shape[1:], 0) + start
        parts = [
            jnp.where(offset < lengths[step * BLOCK + u], block[u].astype(jnp.float32), 0.0)
            for u in range(BLOCK)
        ]
        return jnp.stack(parts).astype(jnp.bfloat16)

    def add_totals(layer, step, block):
        part = pl.ds(pl.multiple_of(step * BLOCK, BLOCK), BLOCK)
        totals[layer, part, :] = dot(user_ones[...], block.reshape(BLOCK * rows, width))

    def mask_step(step, carry):
        event_copy(step).wait()
        part = pl.ds(step * BLOCK, BLOCK)
        block = masked(x[0, part], step, first_pos)
        x[0, part] = block
        add_totals(0, step, block)
        return carry

    lax.fori_loop(0, steps, mask_step, 0)

    def group_copy(layer, k):
        return pltpu.make_async_remote_copy(
            src_ref=totals.at[layer],
            dst_ref=group_got.at[layer, k - 1],
            send_sem=group_send.at[layer, k - 1],
            recv_sem=group_recv.at[layer, k - 1],
            device_id={"tm": group_peer(k)},
            device_id_type=MESH,
        )

    def cross_copy(layer, k):
        return pltpu.make_async_remote_copy(
            src_ref=plane.at[layer],
            dst_ref=cross_got.at[layer, k - 1],
            send_sem=cross_send.at[layer, k - 1],
            recv_sem=cross_recv.at[layer, k - 1],
            device_id={"tm": cross_peer(k)},
            device_id_type=MESH,
        )

    def start_group(layer):
        for k in range(1, group):
            group_copy(layer, k).start()

    def finish_group_start_cross(layer):
        before = jnp.zeros((users, width), jnp.float32)
        whole = totals[layer]
        for k in range(1, group):
            group_copy(layer, k).wait_recv()
            got = group_got[layer, k - 1]
            whole = whole + got
            before = before + jnp.where(in_group >= k, got, 0.0)
        plane[layer] = whole
        earlier[layer] = before
        for k in range(1, groups):

            @pl.when(my_group + k < groups)
            def _(k=k):
                cross_copy(layer, k).start()

    def finish_cross(layer):
        for k in range(1, groups):

            @pl.when(my_group >= k)
            def _(k=k):
                cross_copy(layer, k).wait_recv()
                earlier[layer] += cross_got[layer, k - 1]

    def wait_sum_sends(layer):
        for k in range(1, group):
            group_copy(layer, k).wait_send()
        for k in range(1, groups):

            @pl.when(my_group + k < groups)
            def _(k=k):
                cross_copy(layer, k).wait_send()

    def own_step(layer, step, carry):
        for piece in range(BLOCK // per_dot):
            part = pl.ds(step * BLOCK + piece * per_dot, per_dot)
            block = x[layer, part].reshape(ROWS, width)
            weights = (dot_t(block, block) * own_mask[...]).astype(jnp.bfloat16)
            mixed_own[part] = dot(weights, block).reshape(per_dot, rows, width)
        return carry

    def layer_step(layer, step, carry):
        part = pl.ds(step * BLOCK, BLOCK)
        wait_halos(layer, step)
        block = x[layer, part]
        low_rows, high_rows = low[layer, part], high[layer, part]
        if layer == 0:
            low_rows = masked(low_rows, step, first_pos - HALF)
            high_rows = masked(high_rows, step, first_pos + rows)
        mixed, running = [], []
        for piece in range(BLOCK // per_dot):
            cut = slice(piece * per_dot, (piece + 1) * per_dot)
            here = block[cut].reshape(ROWS, width)
            halo = jnp.concatenate(
                [low_rows[cut].reshape(side_rows, width), high_rows[cut].reshape(side_rows, width)],
                axis=0,
            )
            weights = (dot_t(here, halo) * halo_mask[...]).astype(jnp.bfloat16)
            mixed.append(dot(weights, halo))
            running.append(dot(lower_ones[...], here))
        mixed = jnp.concatenate(mixed, axis=0) + mixed_own[part].reshape(BLOCK * rows, width)
        running = jnp.concatenate(running, axis=0).reshape(BLOCK, rows, width)
        before = earlier[layer, pl.ds(pl.multiple_of(step * BLOCK, BLOCK), BLOCK), :]
        context = (running + before[:, None, :]) * row_scale[...][None]
        context = context.astype(jnp.bfloat16).reshape(BLOCK * rows, width)
        flat = block.reshape(BLOCK * rows, width)
        summed = flat.astype(jnp.float32) + dot(mixed.astype(jnp.bfloat16), mix_v[layer])
        summed = summed + dot(context, ctx_v[layer])
        centered = summed - jnp.mean(summed, axis=-1, keepdims=True)
        variance = jnp.mean(centered * centered, axis=-1, keepdims=True)
        normed = centered * lax.rsqrt(variance + EPS) * gains[layer : layer + 1, :]
        normed = normed.astype(jnp.bfloat16)
        hidden = jnp.maximum(dot(normed, up_v[layer]), 0.0).astype(jnp.bfloat16)
        following = normed.astype(jnp.float32) + dot(hidden, down_v[layer])
        following = masked(following.reshape(BLOCK, rows, width), step, first_pos)
        if layer + 1 < layers:
            x[layer + 1, part] = following
            add_totals(layer + 1, step, following)
            send_halos(layer + 1, step)
        else:
            result[part] = following
            out_copy(step).start()
        return carry

    def out_copy(step):
        part = pl.ds(step * BLOCK, BLOCK)
        return pltpu.make_async_copy(result.at[part], out.at[part], out_sem.at[step])

    for layer in range(layers):
        start_group(layer)
        lax.fori_loop(0, steps // 2, functools.partial(own_step, layer), 0)
        finish_group_start_cross(layer)
        lax.fori_loop(steps // 2, steps, functools.partial(own_step, layer), 0)
        if layer == 0:
            for copy in weight_copies:
                copy.wait()
        finish_cross(layer)
        lax.fori_loop(0, steps, functools.partial(layer_step, layer), 0)

    for layer in range(layers):
        wait_sum_sends(layer)
        for step in range(steps):
            wait_halo_sends(layer, step)
    for step in range(steps):
        out_copy(step).wait()


def per_device(count, events, lengths, w_mix, w_context, gains, w_up, w_down):
    users, rows, width = events.shape
    layers, _, hidden = w_up.shape
    steps = users // BLOCK
    group = group_size(count)
    groups = count // group
    per_dot = ROWS // rows
    bf16, f32 = jnp.bfloat16, jnp.float32
    vmem, dma = pltpu.VMEM, pltpu.SemaphoreType.DMA
    scratch = [
        vmem((layers, users, rows, width), bf16),
        vmem((users, rows, width), bf16),
        vmem((layers, users, HALF, width), bf16),
        vmem((layers, users, HALF, width), bf16),
        vmem((users, rows, width), f32),
        vmem(w_mix.shape, bf16),
        vmem(w_context.shape, bf16),
        vmem(w_up.shape, bf16),
        vmem(w_down.shape, bf16),
        vmem((ROWS, ROWS), f32),
        vmem((ROWS, 2 * per_dot * HALF), f32),
        vmem((ROWS, ROWS), bf16),
        vmem((rows, width), f32),
        vmem((BLOCK, BLOCK * rows), bf16),
        vmem((layers, users, width), f32),
        vmem((layers, group - 1, users, width), f32),
        vmem((layers, users, width), f32),
        vmem((layers, groups - 1, users, width), f32),
        vmem((layers, users, width), f32),
        dma((steps,)),
        dma((4,)),
        dma((steps,)),
        dma((layers, 2, steps)),
        dma((layers, 2, steps)),
        dma((layers, group - 1)),
        dma((layers, group - 1)),
        dma((layers, groups - 1)),
        dma((layers, groups - 1)),
    ]
    anywhere = pl.BlockSpec(memory_space=pl.ANY)
    return pl.pallas_call(
        functools.partial(kernel, count),
        out_shape=jax.ShapeDtypeStruct(events.shape, bf16),
        in_specs=[
            pl.BlockSpec(memory_space=pltpu.SMEM),
            pl.BlockSpec(memory_space=pltpu.VMEM),
        ]
        + [anywhere] * 5,
        out_specs=anywhere,
        scratch_shapes=scratch,
        compiler_params=pltpu.CompilerParams(
            collective_id=0, has_side_effects=True, vmem_limit_bytes=60 * 1024 * 1024
        ),
        name="layers",
    )(lengths, gains, events, w_mix, w_context, w_up, w_down)


def solution(mesh):
    placed = (P("user", "tm", None), P("user"), P(), P(), P(), P(), P())
    return jax.shard_map(
        functools.partial(per_device, mesh.shape["tm"]),
        mesh=mesh,
        in_specs=placed,
        out_specs=P("user", "tm", None),
        check_vma=False,
    )
```

time: 87.3 us -> 48.9 us (0.56)
  the two profiles are of different devices: /device:TPU:0 before, /device:TPU:27 now
where the time goes in v1:
time: 48.9 us; the launch traced here: 48.7 us
  Pallas kernels  46.4 us (95%)
  local copies, waits for them, and re-layouts  2.3 us (5%)
    pallas_call x1, Pallas kernels, per_device(): pl.pallas_call(functools.partial(kernel, count), out_shape=jax.ShapeDtype...  46.4 us
    unnamed x1, local copies, waits for them, and re-layouts  2.3 us

profile of v1, /device:TPU:27, one launch (start us, length us, event | category | flops | bytes accessed | tf_op | source)
XLA Modules:
  0.0 48.7 jit_solution(1922816149338124570)
XLA Ops:
  0.0 46.4 %layers.1 = bf16[32,64,256]{2,1,0:T(8,128)(2,1)} custom-call(s32[32]{0:T(128)} %lengths.1, f32[2,256]{1,0:T(2,128)} %gains.1, bf16[32,64,256]{2,1,0:T(8,128)(2,1)} %events.1, bf16[2,256,256]{2,1,0:T(8,128)(2,1)} %w_mix.1, bf16[2,256,256]{2,1,0:T(8,128)(2,1)} %w_context.1, bf16[2,256,1024]{2,1,0:T(8,128)(2,1)} %w_up.1, bf16[2,1024,256]{2,1,0:T(8,128)(2,1)} %w_down.1), custom_call_target="tpu_custom_call" | custom-call | tf_op jit(solution)/shard_map/layers/pallas_call | solution.py:402
  46.4 2.3 %copy.9 = bf16[32,64,256]{2,1,0:T(8,128)(2,1)} copy(bf16[32,64,256]{2,1,0:T(8,128)(2,1)} %layers.1) | data formatting | bytes 2097152
